TPU v7x, 32 devices: a whole 2x2x4 slice. The times are simulated.
32 devices in a mesh: px: 2 (over x), py: 16 (over z, y, core).
Axes of the slice: x: 2, y: 2, z: 4, core: 2. Of those that a mesh axis runs over, the one named last changes fastest.
Arguments:
- populations: float32 [19, 2, 256, 512], P(None, None, ('py', 'px')), may hold values from 0.02 to 0.12
- pore: int32 [2, 256, 512], P(None, ('py', 'px')), may hold values 0 or 1
Outputs:
- flow: float32 [19, 2, 256, 512], P(None, None, 'py', 'px')
All inputs are finite; a program needn't handle non-finite values. No bound on the sum of `pore` on one device may be relied on, other than what follows from the above.
Results may differ from a plain program's by a relative error of at most 0.0001.
Values sent between devices are 32-bit elements; how exact they have to be, the bound alone decides.
A program may use at most 128 MiB of HBM per device.

v0:
```python
import jax
import jax.numpy as jnp
from jax import lax
from jax.sharding import PartitionSpec as P

STEPS = 2


lattice_velocity = [
    (0, 0, 0),
    (1, 0, 0),
    (-1, 0, 0),
    (0, 1, 0),
    (0, -1, 0),
    (0, 0, 1),
    (0, 0, -1),
    (1, 1, 0),
    (-1, -1, 0),
    (1, -1, 0),
    (-1, 1, 0),
    (1, 0, 1),
    (-1, 0, -1),
    (1, 0, -1),
    (-1, 0, 1),
    (0, 1, 1),
    (0, -1, -1),
    (0, 1, -1),
    (0, -1, 1),
]
lattice_weights = [1.0 / 3.0] + [1.0 / 18.0] * 6 + [1.0 / 36.0] * 12
opposite = [0, 2, 1, 4, 3, 6, 5, 8, 7, 10, 9, 12, 11, 14, 13, 16, 15, 18, 17]
relax_time = 0.8
body_force = 0.005


def with_halo(cells, sides, width):
    for axis, dim in sides:
        count = lax.axis_size(axis)
        head = lax.slice_in_dim(cells, 0, width, axis=dim)
        tail = lax.slice_in_dim(cells, cells.shape[dim] - width, cells.shape[dim], axis=dim)
        cells = jnp.concatenate(
            [
                lax.ppermute(tail, axis, [(i, (i + 1) % count) for i in range(count)]),
                cells,
                lax.ppermute(head, axis, [((i + 1) % count, i) for i in range(count)]),
            ],
            axis=dim,
        )
    return cells


def moment(fields, column):
    total = jnp.zeros_like(fields[0])
    for slot in range(len(lattice_velocity)):
        vector = lattice_velocity[slot]
        if vector[column] != 0:
            total = total + float(vector[column]) * fields[slot]
    return total


def collide(fields, fluid):
    density = jnp.where(fluid > 0.5, jnp.sum(fields, axis=0), 1.0)
    vel_first = moment(fields, 0) / density
    vel_second = moment(fields, 1) / density
    vel_third = moment(fields, 2) / density + relax_time * body_force
    speed = vel_first * vel_first + vel_second * vel_second + vel_third * vel_third
    result = []
    for slot in range(len(lattice_velocity)):
        vector = lattice_velocity[slot]
        along = vector[0] * vel_first + vector[1] * vel_second + vector[2] * vel_third
        equil = (
            lattice_weights[slot]
            * density
            * (1.0 + 3.0 * along + 4.5 * along * along - 1.5 * speed)
        )
        result.append(fields[slot] - (fields[slot] - equil) / relax_time)
    return jnp.stack(result) * fluid[None]


def stream(post, fluid):
    height = post.shape[2]
    width = post.shape[3]
    result = []
    for slot in range(len(lattice_velocity)):
        vector = lattice_velocity[slot]
        rows_from = 1 - vector[1]
        cols_from = 1 - vector[0]
        source = post[
            slot, :, rows_from : height - 2 + rows_from, cols_from : width - 2 + cols_from
        ]
        source = jnp.roll(source, vector[2], axis=0)
        open_cell = fluid[:, rows_from : height - 2 + rows_from, cols_from : width - 2 + cols_from]
        open_cell = jnp.roll(open_cell, vector[2], axis=0)
        bounced = post[opposite[slot], :, 1:-1, 1:-1]
        result.append(jnp.where(open_cell > 0.5, source, bounced))
    return jnp.stack(result) * fluid[None, :, 1:-1, 1:-1]


def body(populations, pore):
    count = populations.shape[0]
    stacked = jnp.concatenate([populations, pore.astype(jnp.float32)[None]], axis=0)
    pencil = lax.all_to_all(stacked, "px", split_axis=3, concat_axis=2, tiled=True)
    fields = pencil[:count]
    padded = with_halo(pencil, (("px", 3), ("py", 2)), 2)
    region = padded[count]
    fields = padded[:count]
    for step in range(STEPS):
        post = collide(fields, region)
        fields = stream(post, region)
        region = region[:, 1:-1, 1:-1]
    return fields


def solution(mesh):
    return jax.shard_map(
        body,
        mesh=mesh,
        in_specs=(P(None, None, ("py", "px"), None), P(None, ("py", "px"), None)),
        out_specs=P(None, None, "py", "px"),
        check_vma=False,
    )
```

profile of v0, /device:TPU:0, one launch (start us, length us, event | category | flops | bytes accessed | tf_op | source)
XLA Modules:
  0.0 70.4 jit_solution(6749811037562610711)
XLA Ops:
  0.0 0.8 %convert_bitcast_fusion = f32[1,2,8,512]{3,2,1,0:T(8,128)S(1)} fusion(s32[2,8,512]{2,1,0:T(8,128)} %param.3), kind=kLoop, calls=%fused_computation.539 | loop fusion | flops 8192 | bytes 65536 | tf_op jit(solution)/shard_map/broadcast_in_dim | solution.py:101
  0.8 1.1 %pad_maximum_fusion.1 = f32[20,2,8,512]{3,2,1,0:T(8,128)S(1)} fusion(f32[1,2,8,512]{3,2,1,0:T(8,128)S(1)} %convert_bitcast_fusion, f32[19,2,8,512]{3,2,1,0:T(8,128)} %param.2), kind=kLoop, calls=%fused_computation.5 | loop fusion | flops 163840 | bytes 1310720 | tf_op jit(solution)/shard_map/concatenate | solution.py:101
  1.9 3.8 %copy.6 = f32[20,2,8,512]{0,2,1,3:T(8,128)} copy(f32[20,2,8,512]{3,2,1,0:T(8,128)S(1)} %pad_maximum_fusion.1) | data formatting | bytes 1310720 | tf_op jit(solution)/shard_map/concatenate | solution.py:101
  5.7 6.0 %reshape.453 = f32[2,1,81920]{2,1,0:T(1,128)S(1)} reshape(f32[512,2,8,20]{3,2,1,0:T(8,128)} %bitcast.557) | data formatting | bytes 1310720
  11.7 13.4 %all_to_all.18 = f32[2,1,81920]{2,1,0:T(1,128)S(1)} all-to-all(f32[2,1,81920]{2,1,0:T(1,128)S(1)} %reshape.453), channel_id=1, replica_groups=mesh['px'=2,'py'=16] {'px'}, dimensions={0} | all-to-all | bytes 1310720 | tf_op jit(solution)/shard_map/all_to_all | solution.py:102
  25.1 0.5 broadcast.1003
  25.6 2.7 %reduce = f32[2,81920]{1,0:T(2,128)S(1)} reduce(f32[2,1,81920]{2,1,0:T(1,128)S(1)} %all_to_all.18, f32[]{:T(128)} %broadcast.1003), dimensions={1}, to_apply=%all_to_all.13.reduce_sub_computation | reduce | bytes 1310724 | tf_op jit(solution)/shard_map/all_to_all | solution.py:102
  28.4 6.9 %reshape.454 = f32[512,2,8,20]{3,2,1,0:T(8,128)} reshape(f32[2,81920]{1,0:T(2,128)S(1)} %reduce) | data formatting | bytes 1310720
  35.3 3.0 %copy.7 = f32[20,2,2,8,256]{4,3,2,1,0:T(8,128)S(1)} copy(f32[20,2,2,8,256]{0,3,1,4,2:T(8,128)} %bitcast.558) | data formatting | bytes 1310720 | tf_op jit(solution)/shard_map/all_to_all | solution.py:102
  38.3 0.2 fusion.285
  38.5 0.3 collective-permute-start
  38.8 1.7 %collective-permute-start.1 = (f32[20,2,16,2]{3,2,1,0:T(8,128)S(1)}, f32[20,2,16,2]{3,2,1,0:T(8,128)S(1)}, u32[]{:S(2)}, u32[]{:S(2)}) collective-permute-start(f32[20,2,16,2]{3,2,1,0:T(8,128)S(1)} %get-tuple-element.82), channel_id=1, source_target_pairs={{16,0},{0,16},{17,1},{1,17},{18,2},{2,18},{19,3},{3,19},{20,4},{4,... | collective-permute-start | bytes 15368 | tf_op jit(solution)/shard_map/ppermute | solution.py:45
  40.6 8.6 %collective-permute-done = f32[20,2,16,2]{3,2,1,0:T(8,128)S(1)} collective-permute-done((f32[20,2,16,2]{3,2,1,0:T(8,128)S(1)}, f32[20,2,16,2]{3,2,1,0:T(8,128)S(1)}, u32[]{:S(2)}, u32[]{:S(2)}) %collective-permute-start) | collective-permute-done | bytes 5152 | tf_op jit(solution)/shard_map/ppermute | solution.py:43
  49.1 4.8 %collective-permute-done.1 = f32[20,2,16,2]{3,2,1,0:T(8,128)S(1)} collective-permute-done((f32[20,2,16,2]{3,2,1,0:T(8,128)S(1)}, f32[20,2,16,2]{3,2,1,0:T(8,128)S(1)}, u32[]{:S(2)}, u32[]{:S(2)}) %collective-permute-start.1) | collective-permute-done | bytes 5152 | tf_op jit(solution)/shard_map/ppermute | solution.py:45
  53.9 0.4 pad_maximum_fusion.4
  54.4 4.4 %collective-permute-start.3 = (f32[20,2,2,260]{3,2,1,0:T(2,128)S(1)}, f32[20,2,2,260]{3,2,1,0:T(2,128)S(1)}, u32[]{:S(2)}, u32[]{:S(2)}) collective-permute-start(f32[20,2,2,260]{3,2,1,0:T(2,128)S(1)} %get-tuple-element.80), channel_id=1, source_target_pairs={{1,0},{2,1},{3,2},{4,3},{5,4},{6,5},{7,6},{8,7},{9,8},{10,9},{11,1... | collective-permute-start | bytes 249608 | tf_op jit(solution)/shard_map/ppermute | solution.py:45
  58.8 2.7 %collective-permute-done.2 = f32[20,2,2,260]{3,2,1,0:T(2,128)S(1)} collective-permute-done((f32[20,2,2,260]{3,2,1,0:T(2,128)S(1)}, f32[20,2,2,260]{3,2,1,0:T(2,128)S(1)}, u32[]{:S(2)}, u32[]{:S(2)}) %collective-permute-start.2) | collective-permute-done | bytes 83232 | tf_op jit(solution)/shard_map/ppermute | solution.py:43
  61.5 0.6 pad_maximum_fusion
  62.2 0.2 constant_dynamic-update-slice_fusion.18
  63.5 0.2 fusion.284
  63.8 0.1 slice_bitcast_fusion.37
  64.2 0.1 constant_dynamic-update-slice_fusion.35
  64.3 0.1 constant_dynamic-update-slice_fusion.34
  64.4 0.1 constant_dynamic-update-slice_fusion.33
  64.9 0.1 constant_dynamic-update-slice_fusion.29
  65.1 0.1 constant_dynamic-update-slice_fusion.27
  66.0 0.1 fusion.282
  66.2 0.2 constant_dynamic-update-slice_fusion.56
  67.3 0.1 broadcast_multiply_fusion
  67.5 0.1 fusion.283
  67.6 0.1 slice_bitcast_fusion.63
  69.5 0.9 %broadcast_multiply_fusion.3 = f32[19,2,16,256]{3,2,1,0:T(8,128)} fusion(f32[19,2,16,256]{3,2,1,0:T(8,128)S(1)} %constant_dynamic-update-slice_fusion.57, f32[2,16,256]{2,1,0:T(8,128)S(1)} %slice.1176), kind=kLoop, calls=%fused_computation.6 | loop fusion | flops 155648 | bytes 1277952 | tf_op jit(solution)/shard_map/mul | solution.py:96
  (77 shorter events, 5.3 us)
Async XLA Ops:
  38.5 10.6 %collective-permute-start = (f32[20,2,16,2]{3,2,1,0:T(8,128)S(1)}, f32[20,2,16,2]{3,2,1,0:T(8,128)S(1)}, u32[]{:S(2)}, u32[]{:S(2)}) collective-permute-start(f32[20,2,16,2]{3,2,1,0:T(8,128)S(1)} %get-tuple-element.81), channel_id=1, source_target_pairs={{0,16},{16,0},{1,17},{17,1},{2,18},{18,2},{3,19},{19,3},{4,20},{20... | collective-permute-start | bytes 15368 | tf_op jit(solution)/shard_map/ppermute | solution.py:43
  38.8 15.1 %collective-permute-start.1 = (f32[20,2,16,2]{3,2,1,0:T(8,128)S(1)}, f32[20,2,16,2]{3,2,1,0:T(8,128)S(1)}, u32[]{:S(2)}, u32[]{:S(2)}) collective-permute-start(f32[20,2,16,2]{3,2,1,0:T(8,128)S(1)} %get-tuple-element.82), channel_id=1, source_target_pairs={{16,0},{0,16},{17,1},{1,17},{18,2},{2,18},{19,3},{3,19},{20,4},{4,... | collective-permute-start | bytes 15368 | tf_op jit(solution)/shard_map/ppermute | solution.py:45
  54.3 7.2 %collective-permute-start.2 = (f32[20,2,2,260]{3,2,1,0:T(2,128)S(1)}, f32[20,2,2,260]{3,2,1,0:T(2,128)S(1)}, u32[]{:S(2)}, u32[]{:S(2)}) collective-permute-start(f32[20,2,2,260]{3,2,1,0:T(2,128)S(1)} %get-tuple-element.79), channel_id=1, source_target_pairs={{0,1},{1,2},{2,3},{3,4},{4,5},{5,6},{6,7},{7,8},{8,9},{9,10},{10,1... | collective-permute-start | bytes 249608 | tf_op jit(solution)/shard_map/ppermute | solution.py:43
  54.4 7.1 %collective-permute-start.3 = (f32[20,2,2,260]{3,2,1,0:T(2,128)S(1)}, f32[20,2,2,260]{3,2,1,0:T(2,128)S(1)}, u32[]{:S(2)}, u32[]{:S(2)}) collective-permute-start(f32[20,2,2,260]{3,2,1,0:T(2,128)S(1)} %get-tuple-element.80), channel_id=1, source_target_pairs={{1,0},{2,1},{3,2},{4,3},{5,4},{6,5},{7,6},{8,7},{9,8},{10,9},{11,1... | collective-permute-start | bytes 249608 | tf_op jit(solution)/shard_map/ppermute | solution.py:45
where the time goes:
time: 70.6 us; the launch traced here: 70.4 us
  local copies, waits for them, and re-layouts  21.5 us (30%)
  waiting for transfers between devices  16 us (23%)
  blocking collectives  13.4 us (19%)
  other arithmetic  12.5 us (18%)
  starting transfers between devices  6.58 us (9%)
    all_to_all x1, blocking collectives, body(): lax.all_to_all(stacked, 'px', split_axis=3, concat_axis=2, tiled=True)  13.4 us
    unnamed x4, local copies, waits for them, and re-layouts  13.1 us
    ppermute x2, waiting for transfers between devices, with_halo(): lax.ppermute(tail, axis, [(i, (i + 1) % count) for i in range(count)])  11.2 us
    ppermute x2, starting transfers between devices, with_halo(): lax.ppermute(head, axis, [((i + 1) % count, i) for i in range(count)])  6.17 us
    unnamed x69, other arithmetic  5.24 us
    ppermute x2, waiting for transfers between devices, with_halo(): lax.ppermute(head, axis, [((i + 1) % count, i) for i in range(count)])  4.76 us
    concatenate x1, local copies, waits for them, and re-layouts, body(): jnp.concatenate([populations, pore.astype(jnp.float32)[None]], axis=0)  3.79 us
    all_to_all x2, local copies, waits for them, and re-layouts, body(): lax.all_to_all(stacked, 'px', split_axis=3, concat_axis=2, tiled=True)  3.53 us
  transfers between devices with their start and end apart: 4, of which 3 were waited for; matrix products, arithmetic and copies ran while one was open for 0% of the time, Pallas kernels for 0%

commit v1 on v0

v1 whole, which is shorter than its diff:
```python
import functools

import jax
import jax.numpy as jnp
from jax import lax
from jax.experimental import pallas as pl
from jax.experimental.pallas import tpu as pltpu
from jax.sharding import PartitionSpec as P

STEPS = 2
MESH = pl.DeviceIdType.MESH

lattice_velocity = [
    (0, 0, 0),
    (1, 0, 0),
    (-1, 0, 0),
    (0, 1, 0),
    (0, -1, 0),
    (0, 0, 1),
    (0, 0, -1),
    (1, 1, 0),
    (-1, -1, 0),
    (1, -1, 0),
    (-1, 1, 0),
    (1, 0, 1),
    (-1, 0, -1),
    (1, 0, -1),
    (-1, 0, 1),
    (0, 1, 1),
    (0, -1, -1),
    (0, 1, -1),
    (0, -1, 1),
]
lattice_weights = [1.0 / 3.0] + [1.0 / 18.0] * 6 + [1.0 / 36.0] * 12
opposite = [0, 2, 1, 4, 3, 6, 5, 8, 7, 10, 9, 12, 11, 14, 13, 16, 15, 18, 17]
relax_time = 0.8
body_force = 0.005

Q = len(lattice_velocity)
LANES = 128
ROWS = 8
HALO = 2
SOLID = -3.0e38


def collide_tile(fields, fluid):
    keep = 1.0 - 1.0 / relax_time
    gain = 1.0 / relax_time
    is_open = fluid > 0.5
    density = functools.reduce(lambda x, y: x + y, fields)
    density = jnp.where(is_open, density, 1.0)
    inverse = 1.0 / density
    vel = []
    for column in range(3):
        plus = [fields[s] for s in range(Q) if lattice_velocity[s][column] > 0]
        minus = [fields[s] for s in range(Q) if lattice_velocity[s][column] < 0]
        total = functools.reduce(lambda x, y: x + y, plus) - functools.reduce(lambda x, y: x + y, minus)
        vel.append(total * inverse)
    vel[2] = vel[2] + relax_time * body_force
    speed = vel[0] * vel[0] + vel[1] * vel[1] + vel[2] * vel[2]
    base = 1.0 - 1.5 * speed
    result = [None] * Q
    scaled = {w: density * (gain * w) for w in sorted(set(lattice_weights))}
    result[0] = jnp.where(is_open, keep * fields[0] + scaled[lattice_weights[0]] * base, SOLID)
    for slot in range(1, Q, 2):
        other = opposite[slot]
        along = None
        for column in range(3):
            sign = lattice_velocity[slot][column]
            if sign == 0:
                continue
            term = vel[column]
            if along is None:
                along = term if sign > 0 else -term
            else:
                along = along + term if sign > 0 else along - term
        weight = scaled[lattice_weights[slot]]
        triple = 3.0 * along
        even = weight * (base + 0.5 * triple * triple)
        odd = weight * triple
        result[slot] = jnp.where(is_open, keep * fields[slot] + (even + odd), SOLID)
        result[other] = jnp.where(is_open, keep * fields[other] + (even - odd), SOLID)
    return result


def kernel(
    across, along, pop_ref, pore_ref, out_ref,
    cells, strip, voxels, packs, edges, post,
    local_sem, a_send, a_recv, b_send, b_recv, e_send, e_recv, h_send, h_recv,
):
    _, planes, rows, _ = pop_ref.shape
    height = across * rows
    width = out_ref.shape[3]
    tall = height + ROWS
    wide = width + LANES
    groups = edges.shape[0]
    per_group = LANES // 4
    me = lax.axis_index("px")
    here = lax.axis_index("py")
    up = lax.rem(here + along - 1, along)
    down = lax.rem(here + 1, along)

    own_rows = pl.ds(pl.multiple_of(me * rows, rows), rows)
    own_cols = pl.ds(pl.multiple_of(me * width, width), width)
    load_pore = pltpu.make_async_copy(pore_ref, voxels, local_sem.at[0])
    load_strip = pltpu.make_async_copy(pop_ref, strip.at[0:Q], local_sem.at[1])
    load_own = pltpu.make_async_copy(
        pop_ref.at[:, :, :, own_cols], cells.at[0:Q, :, own_rows, 0:width], local_sem.at[2]
    )
    load_pore.start()
    load_strip.start()
    load_own.start()

    barrier = pltpu.get_barrier_semaphore()
    for step in range(1, across):
        pl.semaphore_signal(barrier, inc=1, device_id=(lax.rem(me + step, across), here), device_id_type=MESH)
    for to in (up, down):
        pl.semaphore_signal(barrier, inc=1, device_id=(me, to), device_id_type=MESH)

    load_pore.wait()
    strip[Q] = voxels[...].astype(jnp.float32)
    cells[Q, :, own_rows, 0:width] = voxels[:, :, own_cols].astype(jnp.float32)
    load_strip.wait()

    lane = lax.broadcasted_iota(jnp.int32, (rows, LANES), 1)
    total = across * width
    for target in range(across):
        first = (target + 1) * width % total
        last = (target * width - LANES) % total
        for group in range(groups):
            packed = jnp.zeros((rows, LANES), jnp.float32)
            for place in range(per_group):
                slab = group * per_group + place
                if slab >= (Q + 1) * planes:
                    break
                field, plane = slab // planes, slab % planes
                edge = jnp.where(
                    lane < LANES // 2,
                    strip[field, plane, :, first : first + LANES],
                    strip[field, plane, :, last : last + LANES],
                )
                if place == 0:
                    packed = edge
                else:
                    moved = pltpu.roll(edge, 4 * place, 1)
                    packed = jnp.where((lane >= 4 * place - 2) & (lane < 4 * place + 2), moved, packed)
            packs[target, group] = packed
    edges[:, own_rows, :] = packs[me]

    pl.semaphore_wait(barrier, across - 1 + 2)

    def near(source):
        return (rows - HALO, rows) if source == across - 1 else (0, HALO)

    def far(source):
        return (0, rows - HALO) if source == across - 1 else (HALO, rows)

    def strip_copy(source, target, part, send, recv):
        low, high = part(source)
        return pltpu.make_async_remote_copy(
            src_ref=strip.at[:, :, low:high, target * width : (target + 1) * width],
            dst_ref=cells.at[:, :, source * rows + low : source * rows + high, 0:width],
            send_sem=send.at[target],
            recv_sem=recv.at[source],
            device_id=(target, here),
            device_id_type=MESH,
        )

    def edge_copy(source, target):
        return pltpu.make_async_remote_copy(
            src_ref=packs.at[target],
            dst_ref=edges.at[:, source * rows : (source + 1) * rows, :],
            send_sem=e_send.at[target],
            recv_sem=e_recv.at[source],
            device_id=(target, here),
            device_id_type=MESH,
        )

    def halo_copies(way):
        if way == 0:
            source, dest, to = 0, height, up
        else:
            source, dest, to = height - HALO, tall - HALO, down
        return [
            pltpu.make_async_remote_copy(
                src_ref=cells.at[:, :, source : source + HALO, 0:width],
                dst_ref=cells.at[:, :, dest : dest + HALO, 0:width],
                send_sem=h_send.at[2 * way],
                recv_sem=h_recv.at[2 * way],
                device_id=(me, to),
                device_id_type=MESH,
            ),
            pltpu.make_async_remote_copy(
                src_ref=edges.at[:, source : source + HALO, :],
                dst_ref=edges.at[:, dest : dest + HALO, :],
                send_sem=h_send.at[2 * way + 1],
                recv_sem=h_recv.at[2 * way + 1],
                device_id=(me, to),
                device_id_type=MESH,
            ),
        ]

    for mine in range(across):

        @pl.when(me == mine)
        def _():
            others = [(mine + step) % across for step in range(1, across)]
            for target in others:
                strip_copy(mine, target, near, a_send, a_recv).start()
                edge_copy(mine, target).start()
            for target in others:
                strip_copy(mine, target, far, b_send, b_recv).start()
            load_own.wait()
            sources = ((0, 0), (across - 1, 1))
            for source, way in sources:
                if source == mine:
                    for copy in halo_copies(way):
                        copy.start()
            for source, way in sources:
                if source != mine:
                    strip_copy(source, mine, near, a_send, a_recv).wait_recv()
                    edge_copy(source, mine).wait_recv()
                    for copy in halo_copies(way):
                        copy.start()
            for source in others:
                if source not in (0, across - 1):
                    strip_copy(source, mine, near, a_send, a_recv).wait_recv()
                    edge_copy(source, mine).wait_recv()
                strip_copy(source, mine, far, b_send, b_recv).wait_recv()
            for target in others:
                strip_copy(mine, target, near, a_send, a_recv).wait_send()
                edge_copy(mine, target).wait_send()
                strip_copy(mine, target, far, b_send, b_recv).wait_send()
            for way in range(2):
                for copy in halo_copies(way):
                    copy.wait()

    tiles = tall // ROWS

    def unpack(tile, carry):
        at = pl.ds(pl.multiple_of(tile * ROWS, ROWS), ROWS)
        for slab in range((Q + 1) * planes):
            group, place = slab // per_group, slab % per_group
            packed = edges[group, at, :]
            moved = pltpu.roll(packed, LANES - 4 * place, 1) if place else packed
            cells[slab // planes, slab % planes, at, width:wide] = moved
        return carry

    lax.fori_loop(0, tiles, unpack, 0)

    def collide(tile, carry):
        at = pl.ds(pl.multiple_of(tile * ROWS, ROWS), ROWS)
        for plane in range(planes):
            for col in range(0, wide, LANES):
                fields = [cells[slot, plane, at, col : col + LANES] for slot in range(Q)]
                result = collide_tile(fields, cells[Q, plane, at, col : col + LANES])
                for slot in range(Q):
                    post[slot, plane, at, col : col + LANES] = result[slot]
        return carry

    for step in range(STEPS):
        lax.fori_loop(0, tiles, collide, 0)
        for plane in range(planes):
            is_open = cells[Q, plane] > 0.5
            for slot in range(Q):
                vector = lattice_velocity[slot]
                value = post[slot, (plane - vector[2]) % planes]
                if vector[1]:
                    value = pltpu.roll(value, vector[1] % tall, 0)
                if vector[0]:
                    value = pltpu.roll(value, vector[0] % wide, 1)
                if slot:
                    value = jnp.where(value != SOLID, value, post[opposite[slot], plane])
                value = jnp.where(is_open, value, 0.0)
                if step < STEPS - 1:
                    cells[slot, plane] = value
                else:
                    out_ref[slot, plane] = value[:height, :width]


def body(across, along, populations, pore):
    count, planes, rows, columns = populations.shape
    height = across * rows
    width = columns // across
    tall = height + ROWS
    wide = width + LANES
    groups = -(-(count + 1) * planes * 4 // LANES)
    return pl.pallas_call(
        functools.partial(kernel, across, along),
        out_shape=jax.ShapeDtypeStruct((count, planes, height, width), jnp.float32),
        in_specs=[pl.BlockSpec(memory_space=pl.ANY)] * 2,
        out_specs=pl.BlockSpec(memory_space=pltpu.VMEM),
        scratch_shapes=[
            pltpu.VMEM((count + 1, planes, tall, wide), jnp.float32),
            pltpu.VMEM((count + 1, planes, rows, columns), jnp.float32),
            pltpu.VMEM((planes, rows, columns), jnp.int32),
            pltpu.VMEM((across, groups, rows, LANES), jnp.float32),
            pltpu.VMEM((groups, tall, LANES), jnp.float32),
            pltpu.VMEM((count, planes, tall, wide), jnp.float32),
            pltpu.SemaphoreType.DMA((3,)),
            pltpu.SemaphoreType.DMA((across,)),
            pltpu.SemaphoreType.DMA((across,)),
            pltpu.SemaphoreType.DMA((across,)),
            pltpu.SemaphoreType.DMA((across,)),
            pltpu.SemaphoreType.DMA((across,)),
            pltpu.SemaphoreType.DMA((across,)),
            pltpu.SemaphoreType.DMA((4,)),
            pltpu.SemaphoreType.DMA((4,)),
        ],
        compiler_params=pltpu.CompilerParams(collective_id=0, has_side_effects=True),
    )(populations, pore)


def solution(mesh):
    return jax.shard_map(
        functools.partial(body, mesh.shape["px"], mesh.shape["py"]),
        mesh=mesh,
        in_specs=(P(None, None, ("py", "px"), None), P(None, ("py", "px"), None)),
        out_specs=P(None, None, "py", "px"),
        check_vma=False,
    )
```

time: 70.6 us -> 17.8 us (0.25)
  local copies, waits for them, and re-layouts: 21.5 us -> 1.96 us
  waiting for transfers between devices: 16 us -> 0 us
  Pallas kernels: 0 us -> 15.6 us
  blocking collectives: 13.4 us -> 0 us
  other arithmetic: 12.5 us -> 0 us
  starting transfers between devices: 6.58 us -> 0 us
    ppermute x4 -> x0, waiting for transfers between devices: 16 us -> none  [the longest x2 11.2 us: with_halo(): lax.ppermute(tail, axis, [(i, (i + 1) % count) for i in range(count)])]
    pallas_call x0 -> x1, Pallas kernels: none -> 15.6 us  [body(): pl.pallas_call(functools.partial(kernel, across, along), out_shape=jax.Sh...]
    all_to_all x1 -> x0, blocking collectives: 13.4 us -> none  [body(): lax.all_to_all(stacked, 'px', split_axis=3, concat_axis=2, tiled=True)]
    unnamed x4 -> x1, local copies, waits for them, and re-layouts: 13.1 us -> 1.96 us
    ppermute x4 -> x0, starting transfers between devices: 6.58 us -> none  [the longest x2 6.17 us: with_halo(): lax.ppermute(head, axis, [((i + 1) % count, i) for i in range(count)])]
    unnamed x69 -> x0, other arithmetic: 5.24 us -> none
    concatenate x3 -> x0, local copies, waits for them, and re-layouts: 4.05 us -> none  [the longest x1 3.79 us: body(): jnp.concatenate([populations, pore.astype(jnp.float32)[None]], axis=0)]
    all_to_all x2 -> x0, local copies, waits for them, and re-layouts: 3.53 us -> none  [body(): lax.all_to_all(stacked, 'px', split_axis=3, concat_axis=2, tiled=True)]
  transfers between devices with their start and end apart: 4 -> 0, of which waited for: 3 -> 0; matrix products, arithmetic and copies ran while one was open for 0% -> 0% of each run, Pallas kernels for 0% -> 0%
where the time goes in v1:
time: 17.8 us; the launch traced here: 17.6 us
  Pallas kernels  15.6 us (88%)
  local copies, waits for them, and re-layouts  1.96 us (11%)
    pallas_call x1, Pallas kernels, body(): pl.pallas_call(functools.partial(kernel, across, along), out_shape=jax.Sh...  15.6 us
    unnamed x1, local copies, waits for them, and re-layouts  1.96 us

profile of v1, /device:TPU:0, one launch (start us, length us, event | category | flops | bytes accessed | tf_op | source)
XLA Modules:
  0.0 17.6 jit_solution(10100424942832757039)
XLA Ops:
  0.0 15.6 %shard_map.28 = f32[19,2,16,256]{3,2,1,0:T(8,128)} custom-call(f32[19,2,8,512]{3,2,1,0:T(8,128)} %pop_ref.1, s32[2,8,512]{2,1,0:T(8,128)} %pore_ref.1), custom_call_target="tpu_custom_call" | custom-call | tf_op jit(solution)/shard_map/pallas_call | solution.py:288
  15.6 2.0 %copy.4 = f32[19,2,16,256]{3,2,1,0:T(8,128)} copy(f32[19,2,16,256]{3,2,1,0:T(8,128)} %shard_map.28) | data formatting | bytes 1245184

commit v2 on v1

--- a/solution.py
+++ b/solution.py
@@ -40,6 +40,7 @@
 LANES = 128
 ROWS = 8
 HALO = 2
+VMEM_LIMIT = 24 * 1024 * 1024
 SOLID = -3.0e38
 
 
@@ -84,13 +85,13 @@
 
 
 def kernel(
-    across, along, pop_ref, pore_ref, out_ref,
-    cells, strip, voxels, packs, edges, post,
+    across, along, pop_ref, pore_ref, post, mask,
+    cells, strip, voxels, packs, edges,
     local_sem, a_send, a_recv, b_send, b_recv, e_send, e_recv, h_send, h_recv,
 ):
     _, planes, rows, _ = pop_ref.shape
     height = across * rows
-    width = out_ref.shape[3]
+    width = pop_ref.shape[3] // across
     tall = height + ROWS
     wide = width + LANES
     groups = edges.shape[0]
@@ -260,22 +261,40 @@
 
     for step in range(STEPS):
         lax.fori_loop(0, tiles, collide, 0)
+        if step < STEPS - 1:
+            for plane in range(planes):
+                is_open = cells[Q, plane] > 0.5
+                for slot in range(Q):
+                    cells[slot, plane] = streamed(post, is_open, slot, plane)
+    mask[...] = cells[Q]
+
+
+def streamed(post, is_open, slot, plane):
+    _, planes, tall, wide = post.shape
+    vector = lattice_velocity[slot]
+    value = post[slot, (plane - vector[2]) % planes]
+    if vector[1]:
+        value = pltpu.roll(value, vector[1] % tall, 0)
+    if vector[0]:
+        value = pltpu.roll(value, vector[0] % wide, 1)
+    if slot:
+        value = jnp.where(value != SOLID, value, post[opposite[slot], plane])
+    return jnp.where(is_open, value, 0.0)
+
+
+def finish(post, mask, out_ref, flow, sems):
+    _, planes, height, width = flow.shape
+    copies = []
+    for slot in range(Q):
         for plane in range(planes):
-            is_open = cells[Q, plane] > 0.5
-            for slot in range(Q):
-                vector = lattice_velocity[slot]
-                value = post[slot, (plane - vector[2]) % planes]
-                if vector[1]:
-                    value = pltpu.roll(value, vector[1] % tall, 0)
-                if vector[0]:
-                    value = pltpu.roll(value, vector[0] % wide, 1)
-                if slot:
-                    value = jnp.where(value != SOLID, value, post[opposite[slot], plane])
-                value = jnp.where(is_open, value, 0.0)
-                if step < STEPS - 1:
-                    cells[slot, plane] = value
-                else:
-                    out_ref[slot, plane] = value[:height, :width]
+            value = streamed(post, mask[plane] > 0.5, slot, plane)
+            flow[slot, plane] = value[:height, :width]
+        copies.append(pltpu.make_async_copy(flow.at[slot], out_ref.at[slot], sems.at[slot]))
+        if slot:
+            copies[slot - 1].start()
+    copies[-1].start()
+    for copy in copies:
+        copy.wait()
 
 
 def body(across, along, populations, pore):
@@ -285,18 +304,20 @@
     tall = height + ROWS
     wide = width + LANES
     groups = -(-(count + 1) * planes * 4 // LANES)
-    return pl.pallas_call(
+    post, mask = pl.pallas_call(
         functools.partial(kernel, across, along),
-        out_shape=jax.ShapeDtypeStruct((count, planes, height, width), jnp.float32),
-        in_specs=[pl.BlockSpec(memory_space=pl.ANY)] * 2,
-        out_specs=pl.BlockSpec(memory_space=pltpu.VMEM),
+        out_shape=(
+            pltpu.VMEM((count, planes, tall, wide), jnp.float32),
+            pltpu.VMEM((planes, tall, wide), jnp.float32),
+        ),
+        in_specs=[pl.BlockSpec(memory_space=pltpu.HBM)] * 2,
+        out_specs=[pl.BlockSpec(memory_space=pltpu.VMEM)] * 2,
         scratch_shapes=[
             pltpu.VMEM((count + 1, planes, tall, wide), jnp.float32),
             pltpu.VMEM((count + 1, planes, rows, columns), jnp.float32),
             pltpu.VMEM((planes, rows, columns), jnp.int32),
             pltpu.VMEM((across, groups, rows, LANES), jnp.float32),
             pltpu.VMEM((groups, tall, LANES), jnp.float32),
-            pltpu.VMEM((count, planes, tall, wide), jnp.float32),
             pltpu.SemaphoreType.DMA((3,)),
             pltpu.SemaphoreType.DMA((across,)),
             pltpu.SemaphoreType.DMA((across,)),
@@ -307,8 +328,21 @@
             pltpu.SemaphoreType.DMA((4,)),
             pltpu.SemaphoreType.DMA((4,)),
         ],
-        compiler_params=pltpu.CompilerParams(collective_id=0, has_side_effects=True),
-    )(populations, pore)
+        compiler_params=pltpu.CompilerParams(
+            collective_id=0, has_side_effects=True, vmem_limit_bytes=VMEM_LIMIT
+        ),
+    )(*(pltpu.with_memory_space_constraint(x, pltpu.HBM) for x in (populations, pore)))
+    return pl.pallas_call(
+        finish,
+        out_shape=jax.ShapeDtypeStruct((count, planes, height, width), jnp.float32),
+        in_specs=[pl.BlockSpec(memory_space=pltpu.VMEM)] * 2,
+        out_specs=pl.BlockSpec(memory_space=pl.ANY),
+        scratch_shapes=[
+            pltpu.VMEM((count, planes, height, width), jnp.float32),
+            pltpu.SemaphoreType.DMA((count,)),
+        ],
+        compiler_params=pltpu.CompilerParams(vmem_limit_bytes=VMEM_LIMIT),
+    )(post, mask)
 
 
 def solution(mesh):

time: 17.8 us -> 15.8 us (0.89)
  local copies, waits for them, and re-layouts: 1.96 us -> 0 us
    unnamed x1 -> x0, local copies, waits for them, and re-layouts: 1.96 us -> none
    pallas_call x1 -> x2, Pallas kernels: 15.6 us -> 15.7 us  [the longest x1 14.6 us: body(): pl.pallas_call(functools.partial(kernel, across, along), out_shape=(pltpu...]
where the time goes in v2:
time: 15.8 us; the launch traced here: 15.7 us
  Pallas kernels  15.7 us (99%)
    pallas_call x1, Pallas kernels, body(): pl.pallas_call(functools.partial(kernel, across, along), out_shape=(pltpu...  14.6 us
    pallas_call x1, Pallas kernels, body(): pl.pallas_call(finish, out_shape=jax.ShapeDtypeStruct((count, planes, hei...  1.06 us

profile of v2, /device:TPU:0, one launch (start us, length us, event | category | flops | bytes accessed | tf_op | source)
XLA Modules:
  0.0 15.7 jit_solution(2663509210369879171)
XLA Ops:
  0.0 14.6 %shard_map.28 = (f32[19,2,24,384]{3,2,1,0:T(8,128)S(1)}, f32[2,24,384]{2,1,0:T(8,128)S(1)}) custom-call(f32[19,2,8,512]{3,2,1,0:T(8,128)} %pop_ref.1, s32[2,8,512]{2,1,0:T(8,128)} %pore_ref.1), custom_call_target="tpu_custom_call" | custom-call | tf_op jit(solution)/shard_map/pallas_call | solution.py:307
  14.6 1.1 %shard_map.29 = f32[19,2,16,256]{3,2,1,0:T(8,128)} custom-call(f32[19,2,24,384]{3,2,1,0:T(8,128)S(1)} %get-tuple-element.7.post, f32[2,24,384]{2,1,0:T(8,128)S(1)} %get-tuple-element.8.mask), custom_call_target="tpu_custom_call" | custom-call | tf_op jit(solution)/shard_map/pallas_call | solution.py:335

commit v3 on v2

--- a/solution.py
+++ b/solution.py
@@ -104,12 +104,20 @@
     own_rows = pl.ds(pl.multiple_of(me * rows, rows), rows)
     own_cols = pl.ds(pl.multiple_of(me * width, width), width)
     load_pore = pltpu.make_async_copy(pore_ref, voxels, local_sem.at[0])
-    load_strip = pltpu.make_async_copy(pop_ref, strip.at[0:Q], local_sem.at[1])
     load_own = pltpu.make_async_copy(
-        pop_ref.at[:, :, :, own_cols], cells.at[0:Q, :, own_rows, 0:width], local_sem.at[2]
+        pop_ref.at[:, :, :, own_cols], cells.at[0:Q, :, own_rows, 0:width], local_sem.at[1]
     )
+    load_strip = []
+    for step in range(1, across + 1):
+        cols = pl.ds(pl.multiple_of(lax.rem(me + step, across) * width, width), width)
+        load_strip.append(
+            pltpu.make_async_copy(
+                pop_ref.at[:, :, :, cols], strip.at[0:Q, :, :, cols], local_sem.at[1 + step]
+            )
+        )
     load_pore.start()
-    load_strip.start()
+    for copy in load_strip:
+        copy.start()
     load_own.start()
 
     barrier = pltpu.get_barrier_semaphore()
@@ -120,8 +128,86 @@
 
     load_pore.wait()
     strip[Q] = voxels[...].astype(jnp.float32)
-    cells[Q, :, own_rows, 0:width] = voxels[:, :, own_cols].astype(jnp.float32)
-    load_strip.wait()
+    for copy in load_strip[:-1]:
+        copy.wait()
+    pl.semaphore_wait(barrier, across - 1 + 2)
+
+    def near(source):
+        return (rows - HALO, rows) if source == across - 1 else (0, HALO)
+
+    def far(source):
+        return (0, rows - HALO) if source == across - 1 else (HALO, rows)
+
+    def strip_copy(source, target, part, cols, send, recv):
+        low, high = part(source)
+        start = target * width
+        return pltpu.make_async_remote_copy(
+            src_ref=strip.at[:, :, low:high, start + cols[0] : start + cols[1]],
+            dst_ref=cells.at[:, :, source * rows + low : source * rows + high, cols[0] : cols[1]],
+            send_sem=send,
+            recv_sem=recv,
+            device_id=(target, here),
+            device_id_type=MESH,
+        )
+
+    def near_copy(source, target):
+        return strip_copy(source, target, near, (0, width), a_send.at[target], a_recv.at[source])
+
+    pieces = [(col, col + LANES) for col in range(0, width, LANES)]
+
+    def far_copies(source, target):
+        return [
+            strip_copy(source, target, far, cols, b_send.at[target, n], b_recv.at[source, n])
+            for n, cols in enumerate(pieces)
+        ]
+
+    def edge_copy(source, target):
+        return pltpu.make_async_remote_copy(
+            src_ref=packs.at[target],
+            dst_ref=edges.at[:, source * rows : (source + 1) * rows, :],
+            send_sem=e_send.at[target],
+            recv_sem=e_recv.at[source],
+            device_id=(target, here),
+            device_id_type=MESH,
+        )
+
+    def halo_copies(way):
+        if way == 0:
+            source, dest, to = 0, height, up
+        else:
+            source, dest, to = height - HALO, tall - HALO, down
+        return [
+            pltpu.make_async_remote_copy(
+                src_ref=cells.at[:, :, source : source + HALO, 0:width],
+                dst_ref=cells.at[:, :, dest : dest + HALO, 0:width],
+                send_sem=h_send.at[2 * way],
+                recv_sem=h_recv.at[2 * way],
+                device_id=(me, to),
+                device_id_type=MESH,
+            ),
+            pltpu.make_async_remote_copy(
+                src_ref=edges.at[:, source : source + HALO, :],
+                dst_ref=edges.at[:, dest : dest + HALO, :],
+                send_sem=h_send.at[2 * way + 1],
+                recv_sem=h_recv.at[2 * way + 1],
+                device_id=(me, to),
+                device_id_type=MESH,
+            ),
+        ]
+
+    def peers(mine):
+        return [(mine + step) % across for step in range(1, across)]
+
+    def on_each(action):
+        for mine in range(across):
+            pl.when(me == mine)(functools.partial(action, mine))
+
+    def send_near(mine):
+        for target in peers(mine):
+            near_copy(mine, target).start()
+
+    on_each(send_near)
+    load_strip[-1].wait()
 
     lane = lax.broadcasted_iota(jnp.int32, (rows, LANES), 1)
     total = across * width
@@ -146,121 +232,121 @@
                     moved = pltpu.roll(edge, 4 * place, 1)
                     packed = jnp.where((lane >= 4 * place - 2) & (lane < 4 * place + 2), moved, packed)
             packs[target, group] = packed
+
+    ends = ((0, 0), (across - 1, 1))
+
+    def send_rest(mine):
+        for target in peers(mine):
+            edge_copy(mine, target).start()
+        for target in peers(mine):
+            for copy in far_copies(mine, target):
+                copy.start()
+
+    on_each(send_rest)
     edges[:, own_rows, :] = packs[me]
-
-    pl.semaphore_wait(barrier, across - 1 + 2)
-
-    def near(source):
-        return (rows - HALO, rows) if source == across - 1 else (0, HALO)
-
-    def far(source):
-        return (0, rows - HALO) if source == across - 1 else (HALO, rows)
-
-    def strip_copy(source, target, part, send, recv):
-        low, high = part(source)
-        return pltpu.make_async_remote_copy(
-            src_ref=strip.at[:, :, low:high, target * width : (target + 1) * width],
-            dst_ref=cells.at[:, :, source * rows + low : source * rows + high, 0:width],
-            send_sem=send.at[target],
-            recv_sem=recv.at[source],
-            device_id=(target, here),
-            device_id_type=MESH,
-        )
-
-    def edge_copy(source, target):
-        return pltpu.make_async_remote_copy(
-            src_ref=packs.at[target],
-            dst_ref=edges.at[:, source * rows : (source + 1) * rows, :],
-            send_sem=e_send.at[target],
-            recv_sem=e_recv.at[source],
-            device_id=(target, here),
-            device_id_type=MESH,
-        )
-
-    def halo_copies(way):
-        if way == 0:
-            source, dest, to = 0, height, up
-        else:
-            source, dest, to = height - HALO, tall - HALO, down
-        return [
-            pltpu.make_async_remote_copy(
-                src_ref=cells.at[:, :, source : source + HALO, 0:width],
-                dst_ref=cells.at[:, :, dest : dest + HALO, 0:width],
-                send_sem=h_send.at[2 * way],
-                recv_sem=h_recv.at[2 * way],
-                device_id=(me, to),
-                device_id_type=MESH,
-            ),
-            pltpu.make_async_remote_copy(
-                src_ref=edges.at[:, source : source + HALO, :],
-                dst_ref=edges.at[:, dest : dest + HALO, :],
-                send_sem=h_send.at[2 * way + 1],
-                recv_sem=h_recv.at[2 * way + 1],
-                device_id=(me, to),
-                device_id_type=MESH,
-            ),
-        ]
-
-    for mine in range(across):
-
-        @pl.when(me == mine)
-        def _():
-            others = [(mine + step) % across for step in range(1, across)]
-            for target in others:
-                strip_copy(mine, target, near, a_send, a_recv).start()
-                edge_copy(mine, target).start()
-            for target in others:
-                strip_copy(mine, target, far, b_send, b_recv).start()
-            load_own.wait()
-            sources = ((0, 0), (across - 1, 1))
-            for source, way in sources:
-                if source == mine:
-                    for copy in halo_copies(way):
-                        copy.start()
-            for source, way in sources:
-                if source != mine:
-                    strip_copy(source, mine, near, a_send, a_recv).wait_recv()
-                    edge_copy(source, mine).wait_recv()
-                    for copy in halo_copies(way):
-                        copy.start()
-            for source in others:
-                if source not in (0, across - 1):
-                    strip_copy(source, mine, near, a_send, a_recv).wait_recv()
-                    edge_copy(source, mine).wait_recv()
-                strip_copy(source, mine, far, b_send, b_recv).wait_recv()
-            for target in others:
-                strip_copy(mine, target, near, a_send, a_recv).wait_send()
-                edge_copy(mine, target).wait_send()
-                strip_copy(mine, target, far, b_send, b_recv).wait_send()
-            for way in range(2):
-                for copy in halo_copies(way):
-                    copy.wait()
-
-    tiles = tall // ROWS
-
-    def unpack(tile, carry):
+    cells[Q, :, own_rows, 0:width] = voxels[:, :, own_cols].astype(jnp.float32)
+    load_own.wait()
+
+    def unpack(tile):
         at = pl.ds(pl.multiple_of(tile * ROWS, ROWS), ROWS)
         for slab in range((Q + 1) * planes):
             group, place = slab // per_group, slab % per_group
             packed = edges[group, at, :]
             moved = pltpu.roll(packed, LANES - 4 * place, 1) if place else packed
             cells[slab // planes, slab % planes, at, width:wide] = moved
-        return carry
-
-    lax.fori_loop(0, tiles, unpack, 0)
-
-    def collide(tile, carry):
+
+    def collide(tile, columns):
         at = pl.ds(pl.multiple_of(tile * ROWS, ROWS), ROWS)
         for plane in range(planes):
-            for col in range(0, wide, LANES):
+            for col in columns:
                 fields = [cells[slot, plane, at, col : col + LANES] for slot in range(Q)]
                 result = collide_tile(fields, cells[Q, plane, at, col : col + LANES])
                 for slot in range(Q):
                     post[slot, plane, at, col : col + LANES] = result[slot]
+
+    tiles = tall // ROWS
+    per_strip = rows // ROWS
+    all_columns = range(0, wide, LANES)
+
+    def relay_own(mine):
+        for source, way in ends:
+            if source == mine:
+                for copy in halo_copies(way):
+                    copy.start()
+
+    on_each(relay_own)
+    for part in range(per_strip):
+        unpack(me * per_strip + part)
+        collide(me * per_strip + part, all_columns)
+
+    def relay(mine):
+        for source, way in ends:
+            if source != mine:
+                near_copy(source, mine).wait_recv()
+                edge_copy(source, mine).wait_recv()
+                for copy in halo_copies(way):
+                    copy.start()
+        for source in peers(mine):
+            if source not in (0, across - 1):
+                near_copy(source, mine).wait_recv()
+                edge_copy(source, mine).wait_recv()
+
+    on_each(relay)
+
+    def source_at(step):
+        return lax.rem(me + step, across)
+
+    def take_piece(step, n):
+        source = source_at(step)
+        low, high = pieces[n]
+        arrived = cells.at[:, :, 0 : rows - HALO, low:high]
+        pltpu.make_async_copy(arrived, arrived, b_recv.at[source, n]).wait()
+        for part in range(per_strip):
+            collide(source * per_strip + part, (low,))
+
+    def take_edges(step, carry):
+        for part in range(per_strip):
+            unpack(source_at(step) * per_strip + part)
+            collide(source_at(step) * per_strip + part, (width,))
         return carry
 
+    def take_most(step, carry):
+        for n in range(len(pieces) - 1):
+            take_piece(step, n)
+        return carry
+
+    def take_last(step, carry):
+        take_piece(step, len(pieces) - 1)
+        return carry
+
+    lax.fori_loop(1, across, take_edges, 0)
+    lax.fori_loop(1, across, take_most, 0)
+    for way in range(2):
+        for copy in halo_copies(way):
+            copy.wait_recv()
+    unpack(tiles - 1)
+    collide(tiles - 1, all_columns)
+    lax.fori_loop(1, across, take_last, 0)
+
+    def sent(mine):
+        for target in peers(mine):
+            near_copy(mine, target).wait_send()
+            edge_copy(mine, target).wait_send()
+            for copy in far_copies(mine, target):
+                copy.wait_send()
+        for way in range(2):
+            for copy in halo_copies(way):
+                copy.wait_send()
+
+    on_each(sent)
+
+    def collide_all(tile, carry):
+        collide(tile, all_columns)
+        return carry
+
     for step in range(STEPS):
-        lax.fori_loop(0, tiles, collide, 0)
+        if step:
+            lax.fori_loop(0, tiles, collide_all, 0)
         if step < STEPS - 1:
             for plane in range(planes):
                 is_open = cells[Q, plane] > 0.5
@@ -318,11 +404,11 @@
             pltpu.VMEM((planes, rows, columns), jnp.int32),
             pltpu.VMEM((across, groups, rows, LANES), jnp.float32),
             pltpu.VMEM((groups, tall, LANES), jnp.float32),
-            pltpu.SemaphoreType.DMA((3,)),
+            pltpu.SemaphoreType.DMA((2 + across,)),
             pltpu.SemaphoreType.DMA((across,)),
             pltpu.SemaphoreType.DMA((across,)),
-            pltpu.SemaphoreType.DMA((across,)),
-            pltpu.SemaphoreType.DMA((across,)),
+            pltpu.SemaphoreType.DMA((across, width // LANES)),
+            pltpu.SemaphoreType.DMA((across, width // LANES)),
             pltpu.SemaphoreType.DMA((across,)),
             pltpu.SemaphoreType.DMA((across,)),
             pltpu.SemaphoreType.DMA((4,)),

time: 15.8 us -> 15.1 us (0.956)
  Pallas kernels: 15.7 us -> 14.9 us
    pallas_call x1, Pallas kernels: 14.6 us -> 13.8 us  [body(): pl.pallas_call(functools.partial(kernel, across, along), out_shape=(pltpu...]
where the time goes in v3:
time: 15.1 us; the launch traced here: 14.9 us
  Pallas kernels  14.9 us (99%)
    pallas_call x1, Pallas kernels, body(): pl.pallas_call(functools.partial(kernel, across, along), out_shape=(pltpu...  13.8 us
    pallas_call x1, Pallas kernels, body(): pl.pallas_call(finish, out_shape=jax.ShapeDtypeStruct((count, planes, hei...  1.06 us

profile of v3, /device:TPU:0, one launch (start us, length us, event | category | flops | bytes accessed | tf_op | source)
XLA Modules:
  0.0 14.9 jit_solution(14247225170562077641)
XLA Ops:
  0.0 13.8 %shard_map.28 = (f32[19,2,24,384]{3,2,1,0:T(8,128)S(1)}, f32[2,24,384]{2,1,0:T(8,128)S(1)}) custom-call(f32[19,2,8,512]{3,2,1,0:T(8,128)} %pop_ref.1, s32[2,8,512]{2,1,0:T(8,128)} %pore_ref.1), custom_call_target="tpu_custom_call" | custom-call | tf_op jit(solution)/shard_map/pallas_call | solution.py:393
  13.9 1.1 %shard_map.29 = f32[19,2,16,256]{3,2,1,0:T(8,128)} custom-call(f32[19,2,24,384]{3,2,1,0:T(8,128)S(1)} %get-tuple-element.7.post, f32[2,24,384]{2,1,0:T(8,128)S(1)} %get-tuple-element.8.mask), custom_call_target="tpu_custom_call" | custom-call | tf_op jit(solution)/shard_map/pallas_call | solution.py:421

commit v4 on v3

--- a/solution.py
+++ b/solution.py
@@ -87,7 +87,7 @@
 def kernel(
     across, along, pop_ref, pore_ref, post, mask,
     cells, strip, voxels, packs, edges,
-    local_sem, a_send, a_recv, b_send, b_recv, e_send, e_recv, h_send, h_recv,
+    local_sem, a_send, a_recv, b_send, b_recv, e_send, e_recv, h_send, h_recv, w_send,
 ):
     _, planes, rows, _ = pop_ref.shape
     height = across * rows
@@ -126,11 +126,25 @@
     for to in (up, down):
         pl.semaphore_signal(barrier, inc=1, device_id=(me, to), device_id_type=MESH)
 
+    corner = jnp.logical_and(me == across - 1, here == along - 1)
+
+    @pl.when(jnp.logical_and(me != across - 1, here == 0))
+    def _():
+        pl.semaphore_signal(barrier, inc=1, device_id=(across - 1, along - 1), device_id_type=MESH)
+
     load_pore.wait()
     strip[Q] = voxels[...].astype(jnp.float32)
     for copy in load_strip[:-1]:
         copy.wait()
-    pl.semaphore_wait(barrier, across - 1 + 2)
+    greeted = across - 1 + 2
+
+    @pl.when(corner)
+    def _():
+        pl.semaphore_wait(barrier, greeted + across - 1)
+
+    @pl.when(jnp.logical_not(corner))
+    def _():
+        pl.semaphore_wait(barrier, greeted)
 
     def near(source):
         return (rows - HALO, rows) if source == across - 1 else (0, HALO)
@@ -195,6 +209,26 @@
             ),
         ]
 
+    def wrap_rows(target):
+        return pltpu.make_async_remote_copy(
+            src_ref=strip.at[:, :, rows - HALO : rows, target * width : (target + 1) * width],
+            dst_ref=cells.at[:, :, tall - HALO : tall, 0:width],
+            send_sem=w_send.at[0, target],
+            recv_sem=h_recv.at[2],
+            device_id=(target, 0),
+            device_id_type=MESH,
+        )
+
+    def wrap_edges(target):
+        return pltpu.make_async_remote_copy(
+            src_ref=packs.at[target, :, rows - HALO : rows, :],
+            dst_ref=edges.at[:, tall - HALO : tall, :],
+            send_sem=w_send.at[1, target],
+            recv_sem=h_recv.at[3],
+            device_id=(target, 0),
+            device_id_type=MESH,
+        )
+
     def peers(mine):
         return [(mine + step) % across for step in range(1, across)]
 
@@ -205,6 +239,11 @@
     def send_near(mine):
         for target in peers(mine):
             near_copy(mine, target).start()
+
+    @pl.when(corner)
+    def _():
+        for target in range(across - 1):
+            wrap_rows(target).start()
 
     on_each(send_near)
     load_strip[-1].wait()
@@ -242,6 +281,11 @@
             for copy in far_copies(mine, target):
                 copy.start()
 
+    @pl.when(corner)
+    def _():
+        for target in range(across - 1):
+            wrap_edges(target).start()
+
     on_each(send_rest)
     edges[:, own_rows, :] = packs[me]
     cells[Q, :, own_rows, 0:width] = voxels[:, :, own_cols].astype(jnp.float32)
@@ -284,8 +328,12 @@
             if source != mine:
                 near_copy(source, mine).wait_recv()
                 edge_copy(source, mine).wait_recv()
-                for copy in halo_copies(way):
-                    copy.start()
+
+                @pl.when(jnp.logical_or(way == 0, here != along - 1))
+                def _():
+                    for copy in halo_copies(way):
+                        copy.start()
+
         for source in peers(mine):
             if source not in (0, across - 1):
                 near_copy(source, mine).wait_recv()
@@ -334,11 +382,20 @@
             edge_copy(mine, target).wait_send()
             for copy in far_copies(mine, target):
                 copy.wait_send()
-        for way in range(2):
-            for copy in halo_copies(way):
-                copy.wait_send()
+        for source, way in ends:
+
+            @pl.when(jnp.logical_or(way == 0 or source == mine, here != along - 1))
+            def _():
+                for copy in halo_copies(way):
+                    copy.wait_send()
 
     on_each(sent)
+
+    @pl.when(corner)
+    def _():
+        for target in range(across - 1):
+            wrap_rows(target).wait_send()
+            wrap_edges(target).wait_send()
 
     def collide_all(tile, carry):
         collide(tile, all_columns)
@@ -413,6 +470,7 @@
             pltpu.SemaphoreType.DMA((across,)),
             pltpu.SemaphoreType.DMA((4,)),
             pltpu.SemaphoreType.DMA((4,)),
+            pltpu.SemaphoreType.DMA((2, across)),
         ],
         compiler_params=pltpu.CompilerParams(
             collective_id=0, has_side_effects=True, vmem_limit_bytes=VMEM_LIMIT

time: 15.1 us -> 15.1 us (level)
  no operation moved by 1% of the time
where the time goes in v4:
time: 15.1 us; the launch traced here: 15 us
  Pallas kernels  15 us (99%)
    pallas_call x1, Pallas kernels, body(): pl.pallas_call(functools.partial(kernel, across, along), out_shape=(pltpu...  13.9 us
    pallas_call x1, Pallas kernels, body(): pl.pallas_call(finish, out_shape=jax.ShapeDtypeStruct((count, planes, hei...  1.06 us

profile of v4, /device:TPU:0, one launch (start us, length us, event | category | flops | bytes accessed | tf_op | source)
XLA Modules:
  0.0 15.0 jit_solution(896290935209722856)
XLA Ops:
  0.0 13.9 %shard_map.28 = (f32[19,2,24,384]{3,2,1,0:T(8,128)S(1)}, f32[2,24,384]{2,1,0:T(8,128)S(1)}) custom-call(f32[19,2,8,512]{3,2,1,0:T(8,128)} %pop_ref.1, s32[2,8,512]{2,1,0:T(8,128)} %pore_ref.1), custom_call_target="tpu_custom_call" | custom-call | tf_op jit(solution)/shard_map/pallas_call | solution.py:450
  13.9 1.1 %shard_map.29 = f32[19,2,16,256]{3,2,1,0:T(8,128)} custom-call(f32[19,2,24,384]{3,2,1,0:T(8,128)S(1)} %get-tuple-element.7.post, f32[2,24,384]{2,1,0:T(8,128)S(1)} %get-tuple-element.8.mask), custom_call_target="tpu_custom_call" | custom-call | tf_op jit(solution)/shard_map/pallas_call | solution.py:479
